TPU v7x, 32 devices: a whole 2x2x4 slice. The times are simulated.
32 devices in a mesh: groups: 2 (over y), tp: 4 (over x, core), sp: 4 (over z).
Axes of the slice: x: 2, y: 2, z: 4, core: 2. Of those that a mesh axis runs over, the one named last changes fastest.
Arguments:
- query_rows: bfloat16 [4, 128, 4096], P('groups', ('sp', 'tp')), parts along dimension 0, may hold values from -100 to 100
- key_rows: bfloat16 [4, 128, 4096], P('groups', ('sp', 'tp')), parts along dimension 0, may hold values from -4 to 4
- value_rows: bfloat16 [4, 128, 4096], P('groups', ('sp', 'tp')), parts along dimension 0, may hold values from -6 to 6
- residual: bfloat16 [4, 128, 2560], P('groups', 'sp', 'tp'), parts along dimension 0, may hold values from -100 to 100
- modulation: float32 [4, 2560], P(None, 'tp'), may hold values from -3 to 3
- out_weight: bfloat16 [2560, 4096], P('tp', 'sp'), may hold values from -0.375 to 0.375
- up_weight: bfloat16 [2560, 7168], P('sp', 'tp'), may hold values from -0.125 to 0.125
- down_weight: bfloat16 [2560, 7168], P('sp', 'tp'), may hold values from -0.0625 to 0.0625
Outputs:
- block_out: bfloat16 [4, 128, 2560], P('groups', 'sp', 'tp'), parts along dimension 0
There are 2 independent parts, one for each index of `groups`. A program takes and returns all parts, laid end to end along the dimension named above; an argument that names none is the same for every part. Nothing has to cross between parts.
All inputs are finite; a program needn't handle non-finite values.
Results may differ from a plain program's by a relative error of at most 0.0044.
Values may be sent and summed in bfloat16 or wider, within the bound.
A program may use at most 64 MiB of HBM per device.

v0:
```python
import math
import jax
import jax.numpy as jnp
from jax import lax
from jax.sharding import PartitionSpec as P

D = 2560
HEAD_FEATURES = 128


def contract_last(left, right):
    return lax.dot_general(
        left, right, (((1,), (1,)), ((), ())), preferred_element_type=jnp.float32
    )


def attend(query_part, key_part, value_part):
    query_heads, key_heads, value_heads = (
        lax.all_to_all(query_part, "sp", split_axis=2, concat_axis=1, tiled=True),
        lax.all_to_all(key_part, "sp", split_axis=2, concat_axis=1, tiled=True),
        lax.all_to_all(value_part, "sp", split_axis=2, concat_axis=1, tiled=True),
    )
    batches, query_count, local_width = query_heads.shape
    local_heads = local_width // HEAD_FEATURES
    grouped = query_heads.reshape(batches, query_count, local_heads, HEAD_FEATURES)
    score_scale = 1.0 / math.sqrt(HEAD_FEATURES)

    def absorb_block(running, blocks):
        block_keys, block_values = blocks
        highest, row_total, weighted_values = running
        attention_logits = (
            jnp.einsum("bqhd,bkhd->bqhk", grouped, block_keys, preferred_element_type=jnp.float32)
            * score_scale
        )
        raised = jnp.maximum(highest, jnp.max(attention_logits, axis=-1))
        damping = jnp.exp(highest - raised)
        exponent = jnp.exp(attention_logits - raised[..., None])
        row_total = row_total * damping + jnp.sum(exponent, axis=-1)
        weighted_values = weighted_values * damping[..., None] + jnp.einsum(
            "bqhk,bkhd->bqhd",
            exponent.astype(jnp.bfloat16),
            block_values,
            preferred_element_type=jnp.float32,
        )
        return (raised, row_total, weighted_values)

    def scan_step(running, blocks):
        return (absorb_block(running, blocks), None)

    def absorb(running, section):
        key_section, value_section = section
        key_count = key_section.shape[1]
        shaped_keys = key_section.reshape(batches, key_count, local_heads, HEAD_FEATURES)
        shaped_values = value_section.reshape(batches, key_count, local_heads, HEAD_FEATURES)
        if key_count > 512 and key_count % 512 == 0:
            block_count = key_count // 512
            key_blocks = jnp.moveaxis(
                shaped_keys.reshape(batches, block_count, 512, local_heads, HEAD_FEATURES), 1, 0
            )
            value_blocks = jnp.moveaxis(
                shaped_values.reshape(batches, block_count, 512, local_heads, HEAD_FEATURES), 1, 0
            )
            running, unused = lax.scan(scan_step, running, (key_blocks, value_blocks))
            return running
        return absorb_block(running, (shaped_keys, shaped_values))

    starting = (
        jnp.full((batches, query_count, local_heads), -jnp.inf, jnp.float32),
        jnp.zeros((batches, query_count, local_heads), jnp.float32),
        jnp.zeros((batches, query_count, local_heads, HEAD_FEATURES), jnp.float32),
    )
    highest, row_total, weighted_values = absorb(
        starting,
        (
            lax.all_gather(key_heads, "tp", axis=1, tiled=True),
            lax.all_gather(value_heads, "tp", axis=1, tiled=True),
        ),
    )
    normalized = (weighted_values / row_total[..., None]).astype(jnp.bfloat16)
    ordered = normalized.reshape(batches, query_count, local_width)
    return lax.all_to_all(ordered, "sp", split_axis=1, concat_axis=2, tiled=True)


def body(
    query_rows, key_rows, value_rows, residual, modulation, out_weight, up_weight, down_weight
):
    attended = attend(query_rows, key_rows, value_rows)
    stripes = lax.all_gather(attended, "tp", axis=1, tiled=True)
    batches, rows_block, inner_width = stripes.shape
    row_count = batches * rows_block
    flat_rows = stripes.reshape(row_count, inner_width)
    local_width = out_weight.shape[0]
    columns = flat_rows
    projected = contract_last(columns, lax.all_gather(out_weight, "sp", axis=1, tiled=True))
    mixed_rows = (
        residual.reshape(row_count, local_width).astype(jnp.float32) + modulation[0] * projected
    )
    first_sum, second_sum = lax.psum(
        (jnp.sum(mixed_rows, axis=1), jnp.sum(mixed_rows * mixed_rows, axis=1)), "tp"
    )
    row_mean = first_sum / D
    spread = second_sum / D - row_mean * row_mean
    normed = (
        (mixed_rows - row_mean[:, None])
        * lax.rsqrt(spread[:, None] + 1e-06)
        * (1.0 + modulation[2])
        + modulation[1]
    ).astype(jnp.bfloat16)
    gathered = lax.all_gather(normed, "tp", axis=1, tiled=True)
    columns = gathered
    hidden = jnp.dot(
        columns,
        lax.all_gather(up_weight, "sp", axis=0, tiled=True),
        preferred_element_type=jnp.float32,
    )
    active = jax.nn.gelu(hidden, approximate=True).astype(jnp.bfloat16)
    partial_out = contract_last(active, lax.all_gather(down_weight, "sp", axis=0, tiled=True))
    summed = lax.psum_scatter(
        partial_out.astype(jnp.bfloat16), "tp", scatter_dimension=1, tiled=True
    ).astype(jnp.float32)
    result = (mixed_rows + modulation[3] * summed).astype(jnp.bfloat16)
    return result.reshape(batches, rows_block, local_width)


def stationary(
    query_rows, key_rows, value_rows, residual, modulation, out_weight, up_weight, down_weight
):
    both = ("sp", "tp")
    stacked = jnp.stack((query_rows, key_rows, value_rows))
    mine = lax.all_to_all(stacked, both, split_axis=3, concat_axis=2, tiled=True)
    batches, tokens, width = mine.shape[1:]
    local_heads = width // HEAD_FEATURES
    heads = mine.reshape(3, batches, tokens, local_heads, HEAD_FEATURES)
    scores = jnp.einsum(
        "bqhd,bkhd->bhqk", heads[0], heads[1], preferred_element_type=jnp.float32
    ) * (1.0 / math.sqrt(HEAD_FEATURES))
    exponent = jnp.exp(scores - jnp.max(scores, axis=-1, keepdims=True))
    row_total = jnp.sum(exponent, axis=-1)
    weighted = jnp.einsum(
        "bhqk,bkhd->bqhd",
        exponent.astype(jnp.bfloat16),
        heads[2],
        preferred_element_type=jnp.float32,
    )
    attended = (weighted / jnp.swapaxes(row_total, 1, 2)[..., None]).astype(jnp.bfloat16)
    attended = attended.reshape(batches, tokens, width)
    attended = lax.all_gather(attended, "tp", axis=2, tiled=True)
    row_count = batches * tokens
    partial = contract_last(attended.reshape(row_count, -1), out_weight)
    partial = partial.astype(jnp.bfloat16).reshape(batches, tokens, -1)
    projected = lax.psum_scatter(partial, "sp", scatter_dimension=1, tiled=True)
    mixed = residual.astype(jnp.float32) + modulation[0] * projected.astype(jnp.float32)
    first_sum, second_sum = lax.psum((jnp.sum(mixed, axis=2), jnp.sum(mixed * mixed, axis=2)), "tp")
    row_mean = first_sum / D
    spread = second_sum / D - row_mean * row_mean
    normed = (
        (mixed - row_mean[..., None]) * lax.rsqrt(spread[..., None] + 1e-06) * (1.0 + modulation[2])
        + modulation[1]
    ).astype(jnp.bfloat16)
    normed = lax.all_gather(normed, "tp", axis=2, tiled=True)
    normed = lax.all_to_all(normed, "sp", split_axis=2, concat_axis=1, tiled=True)
    hidden = jnp.dot(normed.reshape(row_count, -1), up_weight, preferred_element_type=jnp.float32)
    hidden = hidden.astype(jnp.bfloat16).reshape(batches, tokens, -1)
    hidden = lax.psum_scatter(hidden, "sp", scatter_dimension=1, tiled=True)
    active = jax.nn.gelu(hidden.astype(jnp.float32), approximate=True).astype(jnp.bfloat16)
    active = lax.all_gather(active, "sp", axis=1, tiled=True)
    down = contract_last(active.reshape(row_count, -1), down_weight)
    down = down.astype(jnp.bfloat16).reshape(batches, tokens, -1)
    down = lax.psum_scatter(down, "tp", scatter_dimension=1, tiled=True)
    size = lax.axis_size("tp")
    swap = [(s * size + t, t * size + s) for s in range(size) for t in range(size)]
    down = lax.ppermute(down, ("tp", "sp"), swap)
    return (mixed + modulation[3] * down.astype(jnp.float32)).astype(jnp.bfloat16)


def solution(mesh):
    in_specs = (
        P("groups", ("sp", "tp"), None),
        P("groups", ("sp", "tp"), None),
        P("groups", ("sp", "tp"), None),
        P("groups", "sp", "tp"),
        P(None, "tp"),
        P("tp", "sp"),
        P("sp", "tp"),
        P("sp", "tp"),
    )
    out_specs = P("groups", "sp", "tp")

    def block(*operands):
        sizes = mesh.shape
        rows = operands[0].shape[0] * operands[0].shape[1] * sizes["sp"] * sizes["tp"]
        square = sizes["sp"] == sizes["tp"]
        whole_heads = operands[0].shape[2] % (sizes["sp"] * sizes["tp"] * HEAD_FEATURES) == 0
        few = rows < operands[6].shape[0]
        return (stationary if square and whole_heads and few else body)(*operands)

    return jax.shard_map(block, mesh=mesh, in_specs=in_specs, out_specs=out_specs, check_vma=False)
```

profile of v0, /device:TPU:2, one launch (start us, length us, event | category | flops | bytes accessed | tf_op | source)
XLA Modules:
  0.0 260.4 jit_solution(14532735664056187032)
XLA Ops:
  6.5 0.0 copy-start
  6.5 0.0 all-reduce.6.cloned.1.call-start
  6.5 1.2 pad_maximum_fusion
  7.8 10.7 %copy.54 = bf16[3,2,8,4096]{2,1,0,3:T(2,128)(2,1)} copy(bf16[3,2,8,4096]{3,2,1,0:T(8,128)(2,1)S(1)} %pad_maximum_fusion) | data formatting | bytes 786432 | tf_op jit(solution)/shard_map/stack | solution.py:129
  18.5 17.7 %reshape.59 = bf16[16,2,6144]{2,1,0:T(2,128)(2,1)S(1)} reshape(bf16[4096,3,2,8]{3,2,1,0:T(2,128)(2,1)} %bitcast.39) | data formatting | bytes 786432
  36.2 16.5 %all_to_all.30 = bf16[16,2,6144]{2,1,0:T(2,128)(2,1)S(1)} all-to-all(bf16[16,2,6144]{2,1,0:T(2,128)(2,1)S(1)} %reshape.59), channel_id=1, replica_groups=mesh['groups'=2,'tp'=4,'sp'=4] {'sp','tp'}, dimensions={0} | all-to-all | bytes 786432 | tf_op jit(solution)/shard_map/all_to_all | solution.py:130
  52.7 8.3 %reshape.60 = bf16[4096,3,2,8]{3,2,1,0:T(2,128)(2,1)} reshape(bf16[16,2,6144]{2,1,0:T(2,128)(2,1)S(1)} %all_to_all.30) | data formatting | bytes 786432
  61.0 13.3 %copy.55 = bf16[3,2,8,16,256]{4,2,3,1,0:T(8,128)(2,1)S(1)} copy(bf16[3,2,8,16,256]{2,1,0,4,3:T(2,128)(2,1)} %bitcast.40) | data formatting | bytes 786432 | tf_op jit(solution)/shard_map/all_to_all | solution.py:130
  74.5 0.2 fusion.17
  74.7 0.1 fusion.8
  74.7 0.2 fusion.1
  75.0 0.0 copy-start.4
  75.0 0.0 copy-start.2
  75.0 0.0 copy-start.1
  75.0 0.1 copy.60
  75.1 7.9 %all_gather.9 = bf16[2,128,1024]{2,1,0:T(8,128)(2,1)S(1)} all-gather(bf16[2,128,256]{2,1,0:T(8,128)(2,1)S(1)} %copy.60), channel_id=1, replica_groups=mesh['groups'=2,'tp'=4,'sp'=4] {'tp'}, dimensions={2}, use_global_device_ids=true | all-gather | bytes 655360 | tf_op jit(solution)/shard_map/all_gather | solution.py:147
  83.0 1.9 convolution_convert_fusion.2
  84.9 1.1 copy.61
  86.0 0.0 all-reduce.6.cloned.1.call-update
  86.0 0.0 reduce-scatter.2.cloned.1.call-start
  86.1 0.0 copy-done.4
  86.1 0.6 dynamic-slice
  87.3 0.0 copy-done.2
  87.4 34.9 %all-reduce.6.cloned.1.call-done = bf16[2,128,640]{2,0,1:T(2,128)(2,1)} async-done(((bf16[2,128,640]{2,0,1:T(2,128)(2,1)}), bf16[2,128,640]{2,0,1:T(2,128)(2,1)}) %all-reduce.6.cloned.1.call-update) | async-done | bytes 327696
  122.2 0.9 constant_dynamic-slice_fusion.1
  123.2 0.0 copy-done.1
  123.2 0.1 fusion.15
  123.3 5.9 %all-reduce.2 = (f32[2,32]{1,0:T(2,128)S(1)}, f32[2,32]{1,0:T(2,128)S(1)}) all-reduce(f32[2,32]{1,0:T(2,128)S(1)} %get-tuple-element.6, f32[2,32]{1,0:T(2,128)S(1)} %get-tuple-element.5), channel_id=1, replica_groups=mesh['groups'=2,'tp'=4,'sp'=4] {'tp'}, use_global_device_ids=true, to_apply=%region_6.0 | all-reduce | flops 128 | bytes 1024 | tf_op jit(solution)/shard_map/psum | solution.py:153
  129.3 0.1 add_convert_fusion.1
  129.4 6.0 %all_gather.10 = bf16[2,32,2560]{2,1,0:T(8,128)(2,1)S(1)} all-gather(bf16[2,32,640]{2,1,0:T(8,128)(2,1)S(1)} %add_convert_fusion.1), channel_id=1, replica_groups=mesh['groups'=2,'tp'=4,'sp'=4] {'tp'}, dimensions={2}, use_global_device_ids=true | all-gather | bytes 409600 | tf_op jit(solution)/shard_map/all_gather | solution.py:160
  135.3 2.2 copy.63
  137.5 3.7 %reshape.61 = bf16[4,2,20480]{2,1,0:T(2,128)(2,1)S(1)} reshape(bf16[2560,2,32]{2,1,0:T(2,128)(2,1)} %bitcast.41) | data formatting | bytes 655360
  141.2 14.0 %all_to_all.31 = bf16[4,2,20480]{2,1,0:T(2,128)(2,1)S(1)} all-to-all(bf16[4,2,20480]{2,1,0:T(2,128)(2,1)S(1)} %reshape.61), channel_id=1, replica_groups=mesh['groups'=2,'tp'=4,'sp'=4] {'sp'}, dimensions={0} | all-to-all | bytes 655360 | tf_op jit(solution)/shard_map/all_to_all | solution.py:161
  155.2 1.7 reshape.62
  156.9 3.5 %copy.69 = bf16[2,32,4,640]{3,2,1,0:T(4,128)(2,1)S(1)} copy(bf16[2,32,4,640]{1,0,3,2:T(2,128)(2,1)} %bitcast.42) | data formatting | bytes 655360 | tf_op jit(solution)/shard_map/all_to_all | solution.py:161
  160.5 0.0 copy-done
  160.5 1.8 convolution_convert_fusion
  162.3 0.0 reduce-scatter.2.cloned.1.call-update
  162.3 0.0 all-reduce.8.cloned.1.call-start
  162.4 24.5 %reduce-scatter.2.cloned.1.call-done = bf16[2,32,1792]{2,1,0:T(8,128)(2,1)} async-done(((bf16[2,128,1792]{2,1,0:T(8,128)(2,1)}), bf16[2,32,1792]{2,1,0:T(8,128)(2,1)}) %reduce-scatter.2.cloned.1.call-update) | async-done | bytes 229392 | tf_op jit(solution)/shard_map/reduce_scatter | solution.py:164
  186.8 1.1 fusion.7
  187.9 19.0 %all_gather.11 = bf16[2,128,1792]{2,1,0:T(8,128)(2,1)S(1)} all-gather(bf16[2,32,1792]{2,1,0:T(8,128)(2,1)S(1)} %fusion.7), channel_id=1, replica_groups=mesh['groups'=2,'tp'=4,'sp'=4] {'sp'}, dimensions={1}, use_global_device_ids=true | all-gather | bytes 1146880 | tf_op jit(solution)/shard_map/all_gather | solution.py:166
  206.9 0.0 copy-start.3
  206.9 2.6 convolution_convert_fusion.1
  209.5 1.1 copy.66
  210.5 0.0 all-reduce.8.cloned.1.call-update
  210.6 0.0 copy-done.3
  210.6 0.6 dynamic-slice.2
  211.8 29.9 %all-reduce.8.cloned.1.call-done = bf16[2,128,640]{2,0,1:T(2,128)(2,1)} async-done(((bf16[2,128,640]{2,0,1:T(2,128)(2,1)}), bf16[2,128,640]{2,0,1:T(2,128)(2,1)}) %all-reduce.8.cloned.1.call-update) | async-done | bytes 327696
  241.7 0.9 constant_dynamic-slice_fusion
  242.7 5.8 %collective-permute-start = (bf16[2,32,640]{2,1,0:T(8,128)(2,1)S(1)}, bf16[2,32,640]{2,1,0:T(8,128)(2,1)S(1)}, u32[]{:S(2)}, u32[]{:S(2)}) collective-permute-start(bf16[2,32,640]{2,1,0:T(8,128)(2,1)S(1)} %copy.67), channel_id=1, source_target_pairs={{0,0},{1,4},{2,8},{3,12},{4,1},{5,5},{6,9},{7,13},{8,2},{9,6},{10,... | collective-permute-start | bytes 245768 | tf_op jit(solution)/shard_map/ppermute | solution.py:172
  248.5 4.7 %collective-permute-done = bf16[2,32,640]{2,1,0:T(8,128)(2,1)S(1)} collective-permute-done((bf16[2,32,640]{2,1,0:T(8,128)(2,1)S(1)}, bf16[2,32,640]{2,1,0:T(8,128)(2,1)S(1)}, u32[]{:S(2)}, u32[]{:S(2)}) %collective-permute-start) | collective-permute-done | bytes 81952 | tf_op jit(solution)/shard_map/ppermute | solution.py:172
  253.2 0.7 add_convert_fusion
  (8 shorter events, 0.2 us)
Async XLA Ops:
  6.5 153.9 %copy-start = (bf16[640,1792]{1,0:T(8,128)(2,1)S(1)}, bf16[640,1792]{1,0:T(8,128)(2,1)}, u32[]{:S(2)}) copy-start(bf16[640,1792]{1,0:T(8,128)(2,1)} %param.14) | copy-start | bytes 6881284
  6.5 115.7 %all-reduce.6.cloned.1.call-start = ((), (), s32[]{:S(2)}) async-start(), calls=%async_computation.4 | async-start | bytes 655360
  75.0 11.1 %copy-start.4 = (u32[32]{0:T(128)S(1)}, u32[32]{0:T(128)}, u32[]{:S(2)}) copy-start(u32[32]{0:T(128)} %constant.26) | copy-start | bytes 388
  75.0 12.3 %copy-start.2 = (f32[4,640]{1,0:T(4,128)S(1)}, f32[4,640]{1,0:T(4,128)}, u32[]{:S(2)}) copy-start(f32[4,640]{1,0:T(4,128)} %param.12) | copy-start | bytes 30724
  75.0 48.2 %copy-start.1 = (bf16[2,32,640]{2,1,0:T(8,128)(2,1)S(1)}, bf16[2,32,640]{2,1,0:T(8,128)(2,1)}, u32[]{:S(2)}) copy-start(bf16[2,32,640]{2,1,0:T(8,128)(2,1)} %param.11) | copy-start | bytes 245764
  86.0 100.8 %reduce-scatter.2.cloned.1.call-start = ((), (), s32[]{:S(2)}) async-start(), calls=%async_computation.3 | async-start | bytes 1146880 | tf_op jit(solution)/shard_map/reduce_scatter | solution.py:164
  162.3 79.4 %all-reduce.8.cloned.1.call-start = ((), (), s32[]{:S(2)}) async-start(), calls=%async_computation.5 | async-start | bytes 655360
  206.9 3.7 %copy-start.3 = (u32[32]{0:T(128)S(1)}, u32[32]{0:T(128)}, u32[]{:S(2)}) copy-start(u32[32]{0:T(128)} %constant.30) | copy-start | bytes 388
  242.7 10.5 %collective-permute-start = (bf16[2,32,640]{2,1,0:T(8,128)(2,1)S(1)}, bf16[2,32,640]{2,1,0:T(8,128)(2,1)S(1)}, u32[]{:S(2)}, u32[]{:S(2)}) collective-permute-start(bf16[2,32,640]{2,1,0:T(8,128)(2,1)S(1)} %copy.67), channel_id=1, source_target_pairs={{0,0},{1,4},{2,8},{3,12},{4,1},{5,5},{6,9},{7,13},{8,2},{9,6},{10,... | collective-permute-start | bytes 245768 | tf_op jit(solution)/shard_map/ppermute | solution.py:172
Sparse Core Ops, SparseCore 0:
  86.1 36.0 all-reduce.5
  162.5 24.3 reduce-scatter.1
  210.7 31.0 all-reduce.7
where the time goes:
time: 261 us; the launch traced here: 260 us
  waiting for transfers between devices  94 us (36%)
  blocking collectives  69.1 us (26%)
  local copies, waits for them, and re-layouts  66.7 us (26%)
  between operations  14.6 us (6%)
  matrix products  6.76 us (3%)
  starting transfers between devices  5.85 us (2%)
  other arithmetic  3.33 us (1%)
    unnamed x5, waiting for transfers between devices  64.9 us
    unnamed x18, local copies, waits for them, and re-layouts  34.6 us
    reduce_scatter x1, waiting for transfers between devices, stationary(): hidden = lax.psum_scatter(hidden, 'sp', scatter_dimension=1, tiled=True)  24.5 us
    all_gather x1, blocking collectives, stationary(): active = lax.all_gather(active, 'sp', axis=1, tiled=True)  19 us
    all_to_all x1, blocking collectives, stationary(): lax.all_to_all(stacked, both, split_axis=3, concat_axis=2, tiled=True)  16.5 us
    all_to_all x1, blocking collectives, stationary(): lax.all_to_all(normed, 'sp', split_axis=2, concat_axis=1, tiled=True)  14 us
    all_to_all x1, local copies, waits for them, and re-layouts, stationary(): lax.all_to_all(stacked, both, split_axis=3, concat_axis=2, tiled=True)  13.3 us
    another operation x1, local copies, waits for them, and re-layouts, stationary(): stacked = jnp.stack((query_rows, key_rows, value_rows))  10.7 us
  transfers between devices with their start and end apart: 4, of which 4 were waited for; matrix products, arithmetic and copies ran while one was open for 0% of the time, Pallas kernels for 0%

commit v1 on v0

--- a/solution.py
+++ b/solution.py
@@ -127,7 +127,10 @@
 ):
     both = ("sp", "tp")
     stacked = jnp.stack((query_rows, key_rows, value_rows))
-    mine = lax.all_to_all(stacked, both, split_axis=3, concat_axis=2, tiled=True)
+    mine = jnp.concatenate(
+        lax.all_to_all(jnp.stack(jnp.split(stacked, lax.axis_size(both), axis=3)), both, 0, 0),
+        axis=2,
+    )
     batches, tokens, width = mine.shape[1:]
     local_heads = width // HEAD_FEATURES
     heads = mine.reshape(3, batches, tokens, local_heads, HEAD_FEATURES)

time: 261 us -> 211 us (0.81)
  local copies, waits for them, and re-layouts: 66.7 us -> 16.8 us
    unnamed x18 -> x31, local copies, waits for them, and re-layouts: 34.6 us -> 8.59 us
    all_to_all x1 -> x0, local copies, waits for them, and re-layouts: 13.3 us -> none  [stationary(): lax.all_to_all(stacked, both, split_axis=3, concat_axis=2, tiled=True)]
    another operation x1, local copies, waits for them, and re-layouts: 10.7 us -> 0.01 us  [stationary(): jnp.stack(jnp.split(stacked, lax.axis_size(both), axis=3))]
  transfers between devices with their start and end apart: 4 -> 4, of which waited for: 4 -> 4; matrix products, arithmetic and copies ran while one was open for 0% -> 1% of each run, Pallas kernels for 0% -> 0%
where the time goes in v1:
time: 211 us
  waiting for transfers between devices  94 us (45%)
  blocking collectives  69.1 us (33%)
  local copies, waits for them, and re-layouts  16.8 us (8%)
  between operations  14.7 us (7%)
  matrix products  6.78 us (3%)
  starting transfers between devices  5.85 us (3%)
  other arithmetic  3.33 us (2%)
    unnamed x5, waiting for transfers between devices  64.9 us
    reduce_scatter x1, waiting for transfers between devices, stationary(): hidden = lax.psum_scatter(hidden, 'sp', scatter_dimension=1, tiled=True)  24.5 us
    all_gather x1, blocking collectives, stationary(): active = lax.all_gather(active, 'sp', axis=1, tiled=True)  18.9 us
    all_to_all x1, blocking collectives, stationary(): lax.all_to_all(jnp.stack(jnp.split(stacked, lax.axis_size(both), axis=3))...  16.5 us
    all_to_all x1, blocking collectives, stationary(): lax.all_to_all(normed, 'sp', split_axis=2, concat_axis=1, tiled=True)  14 us
    unnamed x31, local copies, waits for them, and re-layouts  8.59 us
    all_gather x1, blocking collectives, stationary(): attended = lax.all_gather(attended, 'tp', axis=2, tiled=True)  7.85 us
    all_gather x1, blocking collectives, stationary(): normed = lax.all_gather(normed, 'tp', axis=2, tiled=True)  5.96 us
  transfers between devices with their start and end apart: 4, of which 4 were waited for; matrix products, arithmetic and copies ran while one was open for 1% of the time, Pallas kernels for 0%

profile of v1, /device:TPU:2, one launch (start us, length us, event | category | flops | bytes accessed | tf_op | source)
XLA Modules:
  0.0 210.6 jit_solution(6487077089085059324)
XLA Ops:
  6.5 0.0 copy-start
  6.5 0.0 all-reduce.6.cloned.1.call-start
  6.5 1.2 pad_maximum_fusion
  8.0 16.5 %all_to_all.20 = bf16[16,3,2,8,256]{4,3,2,1,0:T(8,128)(2,1)S(1)} all-to-all(bf16[16,3,2,8,256]{4,3,2,1,0:T(8,128)(2,1)S(1)} %constant_dynamic-update-slice_fusion), channel_id=1, replica_groups=mesh['groups'=2,'tp'=4,'sp'=4] {'sp','tp'}, dimensions={0} | all-to-all | bytes 786432 | tf_op jit(solution)/shard_map/all_to_all | solution.py:131
  24.7 0.2 fusion.17
  24.9 0.1 fusion.8
  25.0 0.2 fusion.1
  25.2 0.0 copy-start.4
  25.2 0.0 copy-start.2
  25.2 0.0 copy-start.1
  25.2 0.1 copy.67
  25.4 7.9 %all_gather.9 = bf16[2,128,1024]{2,1,0:T(8,128)(2,1)S(1)} all-gather(bf16[2,128,256]{2,1,0:T(8,128)(2,1)S(1)} %copy.67), channel_id=1, replica_groups=mesh['groups'=2,'tp'=4,'sp'=4] {'tp'}, dimensions={2}, use_global_device_ids=true | all-gather | bytes 655360 | tf_op jit(solution)/shard_map/all_gather | solution.py:150
  33.2 1.9 convolution_convert_fusion.2
  35.1 1.1 copy.68
  36.2 0.0 all-reduce.6.cloned.1.call-update
  36.2 0.0 reduce-scatter.2.cloned.1.call-start
  36.3 0.0 copy-done.4
  36.3 0.6 dynamic-slice
  37.5 0.0 copy-done.2
  37.6 34.9 %all-reduce.6.cloned.1.call-done = bf16[2,128,640]{2,0,1:T(2,128)(2,1)} async-done(((bf16[2,128,640]{2,0,1:T(2,128)(2,1)}), bf16[2,128,640]{2,0,1:T(2,128)(2,1)}) %all-reduce.6.cloned.1.call-update) | async-done | bytes 327696
  72.5 0.9 constant_dynamic-slice_fusion.1
  73.4 0.0 copy-done.1
  73.4 0.1 fusion.15
  73.5 5.9 %all-reduce.2 = (f32[2,32]{1,0:T(2,128)S(1)}, f32[2,32]{1,0:T(2,128)S(1)}) all-reduce(f32[2,32]{1,0:T(2,128)S(1)} %get-tuple-element.6, f32[2,32]{1,0:T(2,128)S(1)} %get-tuple-element.5), channel_id=1, replica_groups=mesh['groups'=2,'tp'=4,'sp'=4] {'tp'}, use_global_device_ids=true, to_apply=%region_6.0 | all-reduce | flops 128 | bytes 1024 | tf_op jit(solution)/shard_map/psum | solution.py:156
  79.5 0.1 add_convert_fusion.1
  79.6 6.0 %all_gather.10 = bf16[2,32,2560]{2,1,0:T(8,128)(2,1)S(1)} all-gather(bf16[2,32,640]{2,1,0:T(8,128)(2,1)S(1)} %add_convert_fusion.1), channel_id=1, replica_groups=mesh['groups'=2,'tp'=4,'sp'=4] {'tp'}, dimensions={2}, use_global_device_ids=true | all-gather | bytes 409600 | tf_op jit(solution)/shard_map/all_gather | solution.py:163
  85.5 2.2 %copy.70 = bf16[2,32,2560]{1,0,2:T(2,128)(2,1)} copy(bf16[2,32,2560]{2,1,0:T(8,128)(2,1)S(1)} %all_gather.10) | data formatting | bytes 655360 | tf_op jit(solution)/shard_map/all_gather | solution.py:163
  87.7 3.7 %reshape.61 = bf16[4,2,20480]{2,1,0:T(2,128)(2,1)S(1)} reshape(bf16[2560,2,32]{2,1,0:T(2,128)(2,1)} %bitcast.100) | data formatting | bytes 655360
  91.4 14.0 %all_to_all.21 = bf16[4,2,20480]{2,1,0:T(2,128)(2,1)S(1)} all-to-all(bf16[4,2,20480]{2,1,0:T(2,128)(2,1)S(1)} %reshape.61), channel_id=1, replica_groups=mesh['groups'=2,'tp'=4,'sp'=4] {'sp'}, dimensions={0} | all-to-all | bytes 655360 | tf_op jit(solution)/shard_map/all_to_all | solution.py:164
  105.4 1.7 reshape.62
  107.1 3.5 %copy.76 = bf16[2,32,4,640]{3,2,1,0:T(4,128)(2,1)S(1)} copy(bf16[2,32,4,640]{1,0,3,2:T(2,128)(2,1)} %bitcast.101) | data formatting | bytes 655360 | tf_op jit(solution)/shard_map/all_to_all | solution.py:164
  110.7 0.0 copy-done
  110.7 1.8 convolution_convert_fusion
  112.5 0.0 reduce-scatter.2.cloned.1.call-update
  112.5 0.0 all-reduce.8.cloned.1.call-start
  112.6 24.5 %reduce-scatter.2.cloned.1.call-done = bf16[2,32,1792]{2,1,0:T(8,128)(2,1)} async-done(((bf16[2,128,1792]{2,1,0:T(8,128)(2,1)}), bf16[2,32,1792]{2,1,0:T(8,128)(2,1)}) %reduce-scatter.2.cloned.1.call-update) | async-done | bytes 229392 | tf_op jit(solution)/shard_map/reduce_scatter | solution.py:167
  137.1 1.1 fusion.7
  138.2 18.9 %all_gather.11 = bf16[2,128,1792]{2,1,0:T(8,128)(2,1)S(1)} all-gather(bf16[2,32,1792]{2,1,0:T(8,128)(2,1)S(1)} %fusion.7), channel_id=1, replica_groups=mesh['groups'=2,'tp'=4,'sp'=4] {'sp'}, dimensions={1}, use_global_device_ids=true | all-gather | bytes 1146880 | tf_op jit(solution)/shard_map/all_gather | solution.py:169
  157.1 0.0 copy-start.3
  157.1 2.6 %convolution_convert_fusion.1 = bf16[256,640]{1,0:T(8,128)(2,1)S(1)} fusion(bf16[256,1792]{1,0:T(8,128)(2,1)S(1)} %bitcast.106, bf16[640,1792]{1,0:T(8,128)(2,1)} %param.15), kind=kOutput, calls=%fused_computation.1 | convolution fusion | flops 587366400 | bytes 3538944 | tf_op jit(solution)/shard_map/dot_general | solution.py:12
  159.7 1.1 copy.73
  160.7 0.0 all-reduce.8.cloned.1.call-update
  160.8 0.0 copy-done.3
  160.8 0.6 dynamic-slice.2
  162.0 30.0 %all-reduce.8.cloned.1.call-done = bf16[2,128,640]{2,0,1:T(2,128)(2,1)} async-done(((bf16[2,128,640]{2,0,1:T(2,128)(2,1)}), bf16[2,128,640]{2,0,1:T(2,128)(2,1)}) %all-reduce.8.cloned.1.call-update) | async-done | bytes 327696
  192.0 0.9 constant_dynamic-slice_fusion
  193.0 5.8 %collective-permute-start = (bf16[2,32,640]{2,1,0:T(8,128)(2,1)S(1)}, bf16[2,32,640]{2,1,0:T(8,128)(2,1)S(1)}, u32[]{:S(2)}, u32[]{:S(2)}) collective-permute-start(bf16[2,32,640]{2,1,0:T(8,128)(2,1)S(1)} %copy.74), channel_id=1, source_target_pairs={{0,0},{1,4},{2,8},{3,12},{4,1},{5,5},{6,9},{7,13},{8,2},{9,6},{10,... | collective-permute-start | bytes 245768 | tf_op jit(solution)/shard_map/ppermute | solution.py:175
  198.7 4.7 %collective-permute-done = bf16[2,32,640]{2,1,0:T(8,128)(2,1)S(1)} collective-permute-done((bf16[2,32,640]{2,1,0:T(8,128)(2,1)S(1)}, bf16[2,32,640]{2,1,0:T(8,128)(2,1)S(1)}, u32[]{:S(2)}, u32[]{:S(2)}) %collective-permute-start) | collective-permute-done | bytes 81952 | tf_op jit(solution)/shard_map/ppermute | solution.py:175
  203.4 0.7 add_convert_fusion
  (27 shorter events, 0.4 us)
Async XLA Ops:
  6.5 104.2 %copy-start = (bf16[640,1792]{1,0:T(8,128)(2,1)S(1)}, bf16[640,1792]{1,0:T(8,128)(2,1)}, u32[]{:S(2)}) copy-start(bf16[640,1792]{1,0:T(8,128)(2,1)} %param.14) | copy-start | bytes 6881284
  6.5 65.9 %all-reduce.6.cloned.1.call-start = ((), (), s32[]{:S(2)}) async-start(), calls=%async_computation.4 | async-start | bytes 655360
  25.2 11.1 %copy-start.4 = (u32[32]{0:T(128)S(1)}, u32[32]{0:T(128)}, u32[]{:S(2)}) copy-start(u32[32]{0:T(128)} %constant.26) | copy-start | bytes 388
  25.2 12.3 %copy-start.2 = (f32[4,640]{1,0:T(4,128)S(1)}, f32[4,640]{1,0:T(4,128)}, u32[]{:S(2)}) copy-start(f32[4,640]{1,0:T(4,128)} %param.12) | copy-start | bytes 30724
  25.2 48.2 %copy-start.1 = (bf16[2,32,640]{2,1,0:T(8,128)(2,1)S(1)}, bf16[2,32,640]{2,1,0:T(8,128)(2,1)}, u32[]{:S(2)}) copy-start(bf16[2,32,640]{2,1,0:T(8,128)(2,1)} %param.11) | copy-start | bytes 245764
  36.2 100.8 %reduce-scatter.2.cloned.1.call-start = ((), (), s32[]{:S(2)}) async-start(), calls=%async_computation.3 | async-start | bytes 1146880 | tf_op jit(solution)/shard_map/reduce_scatter | solution.py:167
  112.5 79.4 %all-reduce.8.cloned.1.call-start = ((), (), s32[]{:S(2)}) async-start(), calls=%async_computation.5 | async-start | bytes 655360
  157.1 3.7 %copy-start.3 = (u32[32]{0:T(128)S(1)}, u32[32]{0:T(128)}, u32[]{:S(2)}) copy-start(u32[32]{0:T(128)} %constant.30) | copy-start | bytes 388
  193.0 10.5 %collective-permute-start = (bf16[2,32,640]{2,1,0:T(8,128)(2,1)S(1)}, bf16[2,32,640]{2,1,0:T(8,128)(2,1)S(1)}, u32[]{:S(2)}, u32[]{:S(2)}) collective-permute-start(bf16[2,32,640]{2,1,0:T(8,128)(2,1)S(1)} %copy.74), channel_id=1, source_target_pairs={{0,0},{1,4},{2,8},{3,12},{4,1},{5,5},{6,9},{7,13},{8,2},{9,6},{10,... | collective-permute-start | bytes 245768 | tf_op jit(solution)/shard_map/ppermute | solution.py:175
Sparse Core Ops, SparseCore 0:
  36.4 36.0 all-reduce.5
  112.7 24.3 reduce-scatter.1
  160.9 31.0 all-reduce.7
